TPU v7x, 256 devices: a 4x2x16 block of a 4x16x16 slice. The times are simulated.
256 devices in a mesh: parts: 2 (over y), samp: 128 (over z, x, core).
Axes of the slice: x: 4, y: 2, z: 16, core: 2. Of those that a mesh axis runs over, the one named last changes fastest.
The devices are a block of a 4x16x16 slice.
Arguments:
- expression: bfloat16 [8192, 20480], P(('parts', 'samp')), parts along dimension 0, may hold values from -24 to 24
- current: bfloat16 [8192, 256], P(('parts', 'samp')), parts along dimension 0, may hold values from -6 to 6
- next_packed: int32 [512, 256], P(('parts', 'samp')), parts along dimension 0, may hold values from -2147483648 to 1789569706, as said below
- covariates: float32 [8192, 64], P(('parts', 'samp')), parts along dimension 0, may hold values from -1 to 1
Outputs:
- scores: float32 [40960, 256], P(('parts', 'samp')), parts along dimension 0
- next_block: bfloat16 [8192, 256], P(('parts', 'samp')), parts along dimension 0
There are 2 independent parts, one for each index of `parts`. A program takes and returns all parts, laid end to end along the dimension named above; each array names one. Nothing has to cross between parts.
Inputs may be any that keep to these rules, and one draw needn't show every extreme that they name: Each word holds the dosages (0, 1 or 2) of 16 consecutive samples of one variant, two bits a sample: sample 16 w + j of variant v in bits 2 j and 2 j + 1 of next_packed[v, w], bit 31 being the sign bit of the int32 word.
All inputs are finite; a program needn't handle non-finite values.
Results may differ from a plain program's by a relative error of at most 0.0004.
Values may be sent and summed in bfloat16 or wider, within the bound.
No kernel may reach another device: no remote copies, remote signals or barrier semaphores. Data moves between devices by JAX's collectives and lax.ppermute only.
A program may use at most 64 MiB of HBM per device.

v0:
```python
import functools
import jax
import jax.numpy as jnp
from jax import lax
from jax.sharding import Mesh
from jax.sharding import PartitionSpec as P

SAMP = ("samp_0", "samp_1", "samp_2")
PARTS_SAMP = ("parts", "samp_0", "samp_1", "samp_2")


def one_axis_at_a_time(array, axes):
    return functools.reduce(lax.psum, axes, array)


def unpack_words(packed_words):
    shifts = 2 * jnp.arange(16, dtype=jnp.int32)
    fields = jnp.bitwise_and(
        lax.shift_right_logical(packed_words[:, :, None], shifts[None, None, :]), 3
    )
    return fields.reshape(packed_words.shape[0], -1).T.astype(jnp.float32)


def over_samples(left, right):
    return lax.dot_general(
        left, right, (((0,), (0,)), ((), ())), preferred_element_type=jnp.float32
    )


def precise_samples(left, right):
    return lax.dot_general(left, right, (((0,), (0,)), ((), ())), precision=lax.Precision.HIGHEST)


def shards(expression, current, next_packed, covariates):
    group_size = lax.axis_size(SAMP)
    samples_all = expression.shape[0] * group_size
    scale_factor = float(samples_all) ** (-0.5)
    regrouped = lax.all_to_all(expression, SAMP, split_axis=1, concat_axis=0, tiled=True)
    scores = (
        over_samples(regrouped, lax.all_gather(current, SAMP, axis=0, tiled=True)) * scale_factor
    )
    packed_words = lax.all_to_all(next_packed, SAMP, split_axis=1, concat_axis=0, tiled=True)
    dosage = unpack_words(packed_words)
    local_totals = jnp.sum(dosage, axis=0)
    local_proj = precise_samples(covariates, dosage)
    local_covsum = jnp.sum(covariates, axis=0)
    totals, projected, cov_sums = (
        one_axis_at_a_time(local_totals, SAMP),
        one_axis_at_a_time(local_proj, SAMP),
        one_axis_at_a_time(local_covsum, SAMP),
    )
    average = totals / samples_all
    loading = projected - cov_sums[:, None] * average[None, :]
    leftover = (
        dosage - average[None, :] - jnp.dot(covariates, loading, precision=lax.Precision.HIGHEST)
    )
    sq_norm = one_axis_at_a_time(jnp.sum(leftover * leftover, axis=0), SAMP)
    next_block = (leftover * lax.rsqrt(sq_norm / samples_all + 1e-05)[None, :]).astype(jnp.bfloat16)
    return (scores, next_block)


def solution(mesh):
    split = Mesh(
        mesh.devices.reshape(mesh.shape["parts"], 16, 4, 2), ("parts", "samp_0", "samp_1", "samp_2")
    )
    in_specs = (P(PARTS_SAMP, None), P(PARTS_SAMP, None), P(PARTS_SAMP, None), P(PARTS_SAMP, None))
    out_specs = (P(PARTS_SAMP, None), P(PARTS_SAMP, None))
    return jax.shard_map(
        shards, mesh=split, in_specs=in_specs, out_specs=out_specs, check_vma=False
    )
```

profile of v0, /device:TPU:33, one launch (start us, length us, event | category | flops | bytes accessed | tf_op | source)
XLA Modules:
  0.0 414.3 jit_solution(10181218120002922908)
XLA Ops:
  8.0 0.8 all_to_all.30
  8.9 0.8 copy.9
  9.6 31.0 %all-to-all-start.1 = ((s32[2,128,2]{2,0,1:T(2,128)}), s32[2,128,2]{2,0,1:T(2,128)S(1)}, u32[]{:S(2)}, u32[]{:S(2)}) async-start(s32[2,128,2]{2,0,1:T(2,128)} %copy.9), calls=%async_computation.1 | async-start | bytes 262144 | tf_op jit(solution)/shard_map/all_to_all | solution.py:42
  40.6 3.6 all_to_all.26
  44.3 2.5 copy.8
  46.8 9.7 %all-to-all-done.1 = s32[2,128,2]{2,0,1:T(2,128)S(1)} async-done(((s32[2,128,2]{2,0,1:T(2,128)}), s32[2,128,2]{2,0,1:T(2,128)S(1)}, u32[]{:S(2)}, u32[]{:S(2)}) %all-to-all-start.1) | async-done | bytes 2080 | tf_op jit(solution)/shard_map/all_to_all | solution.py:42
  56.5 9.1 %all-to-all-start = ((bf16[32,128,160]{2,0,1:T(8,128)(2,1)}), bf16[32,128,160]{2,0,1:T(8,128)(2,1)S(1)}, u32[]{:S(2)}, u32[]{:S(2)}) async-start(bf16[32,128,160]{2,0,1:T(8,128)(2,1)} %copy.8), calls=%async_computation | async-start | bytes 4194304 | tf_op jit(solution)/shard_map/all_to_all | solution.py:38
  65.5 0.1 all-reduce.7.cloned.1.call-start
  65.6 0.1 shift_right_logical.26
  65.7 0.1 copy.11
  65.8 0.1 fusion.3
  65.9 0.9 convolution_bitcast_fusion
  66.8 0.1 all-reduce.7.cloned.1.call-update
  66.8 0.1 all-reduce.9.cloned.1.call-start
  66.9 132.8 %all-reduce.7.cloned.1.call-done = f32[64,256]{1,0:T(8,128)} async-done(((f32[64,256]{1,0:T(8,128)}), f32[64,256]{1,0:T(8,128)}) %all-reduce.7.cloned.1.call-update) | async-done | bytes 65552 | tf_op jit(solution)/shard_map/psum | solution.py:13
  199.7 0.1 all-reduce.9.cloned.1.call-update
  199.8 0.1 all-reduce.11.cloned.1.call-start
  199.8 60.7 %all-reduce.9.cloned.1.call-done = f32[64,256]{1,0:T(8,128)} async-done(((f32[64,256]{1,0:T(8,128)}), f32[64,256]{1,0:T(8,128)}) %all-reduce.9.cloned.1.call-update) | async-done | bytes 65552 | tf_op jit(solution)/shard_map/psum | solution.py:13
  260.6 0.1 all-reduce.11.cloned.1.call-update
  260.6 0.1 all-gather.2.cloned.1.call-start
  260.7 0.6 all-gather.2.cloned.1.call-update
  261.3 0.1 fusion.6
  261.4 24.5 %all-reduce = (f32[256]{0:T(256)S(1)}, f32[64]{0:T(128)S(1)}) all-reduce(f32[256]{0:T(256)S(1)} %fusion.6, f32[64]{0:T(128)S(1)} %reduce_sum.28), channel_id=1, replica_groups=mesh['parts'=2,'samp_0'=16,'samp_1'=4,'samp_2'=2] {'samp_0'}, use_global_device_ids=true, to_apply=%region_1.0 | all-reduce | flops 320 | bytes 2560 | tf_op jit(solution)/shard_map/psum | solution.py:13
  285.9 7.2 %all-reduce.1 = (f32[256]{0:T(256)S(1)}, f32[64]{0:T(128)S(1)}) all-reduce(f32[256]{0:T(256)S(1)} %get-tuple-element.2, f32[64]{0:T(128)S(1)} %get-tuple-element.3), channel_id=1, replica_groups=mesh['parts'=2,'samp_0'=16,'samp_1'=4,'samp_2'=2] {'samp_1'}, use_global_device_ids=true, to_apply=%region_2.0 | all-reduce | flops 320 | bytes 2560 | tf_op jit(solution)/shard_map/psum | solution.py:13
  293.1 13.6 %all-reduce.2 = (f32[256]{0:T(256)S(1)}, f32[64]{0:T(128)S(1)}) all-reduce(f32[256]{0:T(256)S(1)} %get-tuple-element.4, f32[64]{0:T(128)S(1)} %get-tuple-element.5), channel_id=1, replica_groups=mesh['parts'=2,'samp_0'=16,'samp_1'=4,'samp_2'=2] {'samp_2'}, use_global_device_ids=true, to_apply=%region_3.0 | all-reduce | flops 320 | bytes 2560 | tf_op jit(solution)/shard_map/psum | solution.py:13
  306.6 1.1 multiply_reduce_fusion
  307.7 22.7 %psum.93 = f32[256]{0:T(256)S(1)} all-reduce(f32[256]{0:T(256)S(1)} %get-tuple-element.8), channel_id=1, replica_groups=mesh['parts'=2,'samp_0'=16,'samp_1'=4,'samp_2'=2] {'samp_0'}, use_global_device_ids=true, to_apply=%region_12.0 | all-reduce | flops 256 | bytes 2048 | tf_op jit(solution)/shard_map/psum | solution.py:13
  330.4 6.8 %psum.94 = f32[256]{0:T(256)S(1)} all-reduce(f32[256]{0:T(256)S(1)} %psum.93), channel_id=1, replica_groups=mesh['parts'=2,'samp_0'=16,'samp_1'=4,'samp_2'=2] {'samp_1'}, use_global_device_ids=true, to_apply=%region_13.0 | all-reduce | flops 256 | bytes 2048 | tf_op jit(solution)/shard_map/psum | solution.py:13
  337.3 9.7 %psum.95 = f32[256]{0:T(256)S(1)} all-reduce(f32[256]{0:T(256)S(1)} %psum.94), channel_id=1, replica_groups=mesh['parts'=2,'samp_0'=16,'samp_1'=4,'samp_2'=2] {'samp_2'}, use_global_device_ids=true, to_apply=%region_14.0 | all-reduce | flops 256 | bytes 2048 | tf_op jit(solution)/shard_map/psum | solution.py:13
  347.0 0.6 fusion.7
  347.6 56.6 %all-gather.2.cloned.1.call-done = bf16[4096,256]{1,0:T(8,128)(2,1)} async-done(((bf16[32,256]{1,0:T(8,128)(2,1)}), bf16[4096,256]{1,0:T(8,128)(2,1)}) %all-gather.2.cloned.1.call-update) | async-done | bytes 2097168 | tf_op jit(solution)/shard_map/all_gather | solution.py:40
  404.2 3.0 convolution_multiply_fusion
  (9 shorter events, 0.1 us)
Async XLA Ops:
  9.6 46.8 %all-to-all-start.1 = ((s32[2,128,2]{2,0,1:T(2,128)}), s32[2,128,2]{2,0,1:T(2,128)S(1)}, u32[]{:S(2)}, u32[]{:S(2)}) async-start(s32[2,128,2]{2,0,1:T(2,128)} %copy.9), calls=%async_computation.1 | async-start | bytes 262144 | tf_op jit(solution)/shard_map/all_to_all | solution.py:42
  46.8 19.1 %copy-start = (f32[32,64]{1,0:T(8,128)S(1)}, f32[32,64]{1,0:T(8,128)}, u32[]{:S(2)}) copy-start(f32[32,64]{1,0:T(8,128)} %param.7) | copy-start | bytes 24580
  56.5 347.7 %all-to-all-start = ((bf16[32,128,160]{2,0,1:T(8,128)(2,1)}), bf16[32,128,160]{2,0,1:T(8,128)(2,1)S(1)}, u32[]{:S(2)}, u32[]{:S(2)}) async-start(bf16[32,128,160]{2,0,1:T(8,128)(2,1)} %copy.8), calls=%async_computation | async-start | bytes 4194304 | tf_op jit(solution)/shard_map/all_to_all | solution.py:38
  65.5 134.2 %all-reduce.7.cloned.1.call-start = ((), (), s32[]{:S(2)}) async-start(), calls=%async_computation.3 | async-start | bytes 131072 | tf_op jit(solution)/shard_map/psum | solution.py:13
  66.8 193.7 %all-reduce.9.cloned.1.call-start = ((), (), s32[]{:S(2)}) async-start(), calls=%async_computation.4 | async-start | bytes 131072 | tf_op jit(solution)/shard_map/psum | solution.py:13
  199.8 106.9 %all-reduce.11.cloned.1.call-start = ((), (), s32[]{:S(2)}) async-start(), calls=%async_computation.5 | async-start | bytes 131072 | tf_op jit(solution)/shard_map/psum | solution.py:13
  260.6 143.6 %all-gather.2.cloned.1.call-start = ((), (), s32[]{:S(2)}) async-start(), calls=%async_computation.2 | async-start | bytes 2113536 | tf_op jit(solution)/shard_map/all_gather | solution.py:40
Sparse Core Ops, SparseCore 0:
  69.3 130.3 all-reduce.6
  202.0 58.4 all-reduce.8
  263.1 39.1 all-reduce.10
Sparse Core Ops, SparseCore 1:
  263.7 140.4 all-gather.1
where the time goes:
time: 415 us; the launch traced here: 414 us
  waiting for transfers between devices  261 us (63%)
  blocking collectives  84.5 us (20%)
  starting transfers between devices  40.3 us (10%)
  between operations  15.3 us (4%)
  local copies, waits for them, and re-layouts  7.9 us (2%)
  matrix products  4.96 us (1%)
    psum x3, waiting for transfers between devices, one_axis_at_a_time(): return functools.reduce(lax.psum, axes, array)  194 us
    psum x6, blocking collectives, one_axis_at_a_time(): return functools.reduce(lax.psum, axes, array)  84.5 us
    all_gather x1, waiting for transfers between devices, shards(): lax.all_gather(current, SAMP, axis=0, tiled=True)  56.6 us
    all_to_all x1, starting transfers between devices, shards(): lax.all_to_all(next_packed, SAMP, split_axis=1, concat_axis=0, tiled=True)  31 us
    all_to_all x1, waiting for transfers between devices, shards(): lax.all_to_all(next_packed, SAMP, split_axis=1, concat_axis=0, tiled=True)  9.66 us
    all_to_all x1, starting transfers between devices, shards(): lax.all_to_all(expression, SAMP, split_axis=1, concat_axis=0, tiled=True)  9.06 us
  transfers between devices with their start and end apart: 6, of which 4 were waited for; matrix products, arithmetic and copies ran while one was open for 1% of the time, Pallas kernels for 0%

commit v1 on v0

--- a/solution.py
+++ b/solution.py
@@ -37,7 +37,13 @@
     scale_factor = float(samples_all) ** (-0.5)
     regrouped = lax.all_to_all(expression, SAMP, split_axis=1, concat_axis=0, tiled=True)
     scores = (
-        over_samples(regrouped, lax.all_gather(current, SAMP, axis=0, tiled=True)) * scale_factor
+        over_samples(
+            regrouped,
+            jnp.concatenate(
+                lax.all_to_all(jnp.stack([current] * lax.axis_size(SAMP)), SAMP, 0, 0), axis=0
+            ),
+        )
+        * scale_factor
     )
     packed_words = lax.all_to_all(next_packed, SAMP, split_axis=1, concat_axis=0, tiled=True)
     dosage = unpack_words(packed_words)

time: 415 us -> 470 us (1.13)
  blocking collectives: 84.5 us -> 200 us
  waiting for transfers between devices: 261 us -> 193 us
    all_to_all x0 -> x1, blocking collectives: none -> 105 us  [shards(): lax.all_to_all(expression, SAMP, split_axis=1, concat_axis=0, tiled=True)]
    all_gather x1 -> x0, waiting for transfers between devices: 56.6 us -> none  [shards(): lax.all_gather(current, SAMP, axis=0, tiled=True)]
    psum x6, blocking collectives: 84.5 us -> 95.4 us  [one_axis_at_a_time(): return functools.reduce(lax.psum, axes, array)]
    psum x3, waiting for transfers between devices: 194 us -> 183 us  [one_axis_at_a_time(): return functools.reduce(lax.psum, axes, array)]
  transfers between devices with their start and end apart: 6 -> 5, of which waited for: 4 -> 4; matrix products, arithmetic and copies ran while one was open for 1% -> 2% of each run, Pallas kernels for 0% -> 0%
where the time goes in v1:
time: 470 us; the launch traced here: 469 us
  blocking collectives  200 us (43%)
  waiting for transfers between devices  193 us (41%)
  starting transfers between devices  43.6 us (9%)
  between operations  13.9 us (3%)
  local copies, waits for them, and re-layouts  11.5 us (2%)
  matrix products  6.64 us (1%)
    psum x3, waiting for transfers between devices, one_axis_at_a_time(): return functools.reduce(lax.psum, axes, array)  183 us
    all_to_all x1, blocking collectives, shards(): lax.all_to_all(expression, SAMP, split_axis=1, concat_axis=0, tiled=True)  105 us
    psum x6, blocking collectives, one_axis_at_a_time(): return functools.reduce(lax.psum, axes, array)  95.4 us
    all_to_all x1, starting transfers between devices, shards(): lax.all_to_all(next_packed, SAMP, split_axis=1, concat_axis=0, tiled=True)  31 us
    all_to_all x1, starting transfers between devices, shards(): lax.all_to_all(jnp.stack([current] * lax.axis_size(SAMP)), SAMP, 0, 0)  12.4 us
    all_to_all x1, waiting for transfers between devices, shards(): lax.all_to_all(next_packed, SAMP, split_axis=1, concat_axis=0, tiled=True)  9.65 us
  transfers between devices with their start and end apart: 5, of which 4 were waited for; matrix products, arithmetic and copies ran while one was open for 2% of the time, Pallas kernels for 0%

profile of v1, /device:TPU:33, one launch (start us, length us, event | category | flops | bytes accessed | tf_op | source)
XLA Modules:
  0.0 469.2 jit_solution(4419667494863788325)
XLA Ops:
  7.2 0.8 all_to_all.31
  8.0 0.8 copy.11
  8.8 31.0 %all-to-all-start.2 = ((s32[2,128,2]{2,0,1:T(2,128)}), s32[2,128,2]{2,0,1:T(2,128)S(1)}, u32[]{:S(2)}, u32[]{:S(2)}) async-start(s32[2,128,2]{2,0,1:T(2,128)} %copy.11), calls=%async_computation.2 | async-start | bytes 262144 | tf_op jit(solution)/shard_map/all_to_all | solution.py:48
  39.8 3.6 all_to_all.27
  43.4 2.5 copy.8
  46.0 9.6 %all-to-all-done.2 = s32[2,128,2]{2,0,1:T(2,128)S(1)} async-done(((s32[2,128,2]{2,0,1:T(2,128)}), s32[2,128,2]{2,0,1:T(2,128)S(1)}, u32[]{:S(2)}, u32[]{:S(2)}) %all-to-all-start.2) | async-done | bytes 2080 | tf_op jit(solution)/shard_map/all_to_all | solution.py:48
  55.6 104.6 %all_to_all.37 = bf16[32,128,160]{2,0,1:T(8,128)(2,1)S(1)} all-to-all(bf16[32,128,160]{2,0,1:T(8,128)(2,1)} %copy.8), channel_id=1, replica_groups=mesh['parts'=2,'samp_0'=16,'samp_1'=4,'samp_2'=2] {'samp_0','samp_1','sa..., dimensions={1} | all-to-all | bytes 2621440 | tf_op jit(solution)/shard_map/all_to_all | solution.py:38
  160.2 1.6 stack.2
  161.7 12.4 %all-to-all-start.1 = ((bf16[128,32,256]{2,1,0:T(8,128)(2,1)}), bf16[128,32,256]{2,1,0:T(8,128)(2,1)}, u32[]{:S(2)}, u32[]{:S(2)}) async-start(bf16[128,32,256]{2,1,0:T(8,128)(2,1)} %stack.2), calls=%async_computation.1 | async-start | bytes 4194304 | tf_op jit(solution)/shard_map/all_to_all | solution.py:43
  174.1 0.1 all-reduce.7.cloned.1.call-start
  174.2 0.1 shift_right_logical.26
  174.3 0.1 copy.13
  174.4 0.1 fusion.16
  174.5 0.9 convolution_bitcast_fusion
  175.4 0.1 all-reduce.7.cloned.1.call-update
  175.4 0.1 all-reduce.9.cloned.1.call-start
  175.5 132.9 %all-reduce.7.cloned.1.call-done = f32[64,256]{1,0:T(8,128)} async-done(((f32[64,256]{1,0:T(8,128)}), f32[64,256]{1,0:T(8,128)}) %all-reduce.7.cloned.1.call-update) | async-done | bytes 65552 | tf_op jit(solution)/shard_map/psum | solution.py:13
  308.3 0.1 all-reduce.9.cloned.1.call-update
  308.4 0.1 all-reduce.11.cloned.1.call-start
  308.5 0.1 fusion.19
  308.6 21.6 %all-reduce = (f32[256]{0:T(256)S(1)}, f32[64]{0:T(128)S(1)}) all-reduce(f32[256]{0:T(256)S(1)} %fusion.19, f32[64]{0:T(128)S(1)} %reduce_sum.28), channel_id=1, replica_groups=mesh['parts'=2,'samp_0'=16,'samp_1'=4,'samp_2'=2] {'samp_0'}, use_global_device_ids=true, to_apply=%region_1.0 | all-reduce | flops 320 | bytes 2560 | tf_op jit(solution)/shard_map/psum | solution.py:13
  330.2 8.8 %all-reduce.1 = (f32[256]{0:T(256)S(1)}, f32[64]{0:T(128)S(1)}) all-reduce(f32[256]{0:T(256)S(1)} %get-tuple-element.2, f32[64]{0:T(128)S(1)} %get-tuple-element.3), channel_id=1, replica_groups=mesh['parts'=2,'samp_0'=16,'samp_1'=4,'samp_2'=2] {'samp_1'}, use_global_device_ids=true, to_apply=%region_2.0 | all-reduce | flops 320 | bytes 2560 | tf_op jit(solution)/shard_map/psum | solution.py:13
  339.0 21.7 %all-reduce.2 = (f32[256]{0:T(256)S(1)}, f32[64]{0:T(128)S(1)}) all-reduce(f32[256]{0:T(256)S(1)} %get-tuple-element.4, f32[64]{0:T(128)S(1)} %get-tuple-element.5), channel_id=1, replica_groups=mesh['parts'=2,'samp_0'=16,'samp_1'=4,'samp_2'=2] {'samp_2'}, use_global_device_ids=true, to_apply=%region_3.0 | all-reduce | flops 320 | bytes 2560 | tf_op jit(solution)/shard_map/psum | solution.py:13
  360.7 8.5 %all-reduce.9.cloned.1.call-done = f32[64,256]{1,0:T(8,128)} async-done(((f32[64,256]{1,0:T(8,128)}), f32[64,256]{1,0:T(8,128)}) %all-reduce.9.cloned.1.call-update) | async-done | bytes 65552 | tf_op jit(solution)/shard_map/psum | solution.py:13
  369.3 41.7 %all-reduce.11.cloned.1.call-done = f32[64,256]{1,0:T(8,128)} async-done(((f32[64,256]{1,0:T(8,128)}), f32[64,256]{1,0:T(8,128)}) %all-reduce.11.cloned.1.call-update) | async-done | bytes 65552 | tf_op jit(solution)/shard_map/psum | solution.py:13
  411.0 1.1 multiply_reduce_fusion
  412.1 23.9 %psum.93 = f32[256]{0:T(256)S(1)} all-reduce(f32[256]{0:T(256)S(1)} %get-tuple-element.8), channel_id=1, replica_groups=mesh['parts'=2,'samp_0'=16,'samp_1'=4,'samp_2'=2] {'samp_0'}, use_global_device_ids=true, to_apply=%region_12.0 | all-reduce | flops 256 | bytes 2048 | tf_op jit(solution)/shard_map/psum | solution.py:13
  436.0 8.4 %psum.94 = f32[256]{0:T(256)S(1)} all-reduce(f32[256]{0:T(256)S(1)} %psum.93), channel_id=1, replica_groups=mesh['parts'=2,'samp_0'=16,'samp_1'=4,'samp_2'=2] {'samp_1'}, use_global_device_ids=true, to_apply=%region_13.0 | all-reduce | flops 256 | bytes 2048 | tf_op jit(solution)/shard_map/psum | solution.py:13
  444.4 11.0 %psum.95 = f32[256]{0:T(256)S(1)} all-reduce(f32[256]{0:T(256)S(1)} %psum.94), channel_id=1, replica_groups=mesh['parts'=2,'samp_0'=16,'samp_1'=4,'samp_2'=2] {'samp_2'}, use_global_device_ids=true, to_apply=%region_14.0 | all-reduce | flops 256 | bytes 2048 | tf_op jit(solution)/shard_map/psum | solution.py:13
  455.4 0.6 fusion.20
  456.0 2.0 copy.9
  458.0 4.6 fusion.8
  (11 shorter events, 0.1 us)
Async XLA Ops:
  8.8 46.8 %all-to-all-start.2 = ((s32[2,128,2]{2,0,1:T(2,128)}), s32[2,128,2]{2,0,1:T(2,128)S(1)}, u32[]{:S(2)}, u32[]{:S(2)}) async-start(s32[2,128,2]{2,0,1:T(2,128)} %copy.11), calls=%async_computation.2 | async-start | bytes 262144 | tf_op jit(solution)/shard_map/all_to_all | solution.py:48
  46.0 114.2 %copy-start.1 = (bf16[32,256]{1,0:T(8,128)(2,1)S(1)}, bf16[32,256]{1,0:T(8,128)(2,1)}, u32[]{:S(2)}) copy-start(bf16[32,256]{1,0:T(8,128)(2,1)} %param.5) | copy-start | bytes 49156
  161.7 12.7 %copy-start = (f32[32,64]{1,0:T(8,128)S(1)}, f32[32,64]{1,0:T(8,128)}, u32[]{:S(2)}) copy-start(f32[32,64]{1,0:T(8,128)} %param.7) | copy-start | bytes 24580
  161.7 296.3 %all-to-all-start.1 = ((bf16[128,32,256]{2,1,0:T(8,128)(2,1)}), bf16[128,32,256]{2,1,0:T(8,128)(2,1)}, u32[]{:S(2)}, u32[]{:S(2)}) async-start(bf16[128,32,256]{2,1,0:T(8,128)(2,1)} %stack.2), calls=%async_computation.1 | async-start | bytes 4194304 | tf_op jit(solution)/shard_map/all_to_all | solution.py:43
  174.1 134.2 %all-reduce.7.cloned.1.call-start = ((), (), s32[]{:S(2)}) async-start(), calls=%async_computation.3 | async-start | bytes 131072 | tf_op jit(solution)/shard_map/psum | solution.py:13
  175.4 193.8 %all-reduce.9.cloned.1.call-start = ((), (), s32[]{:S(2)}) async-start(), calls=%async_computation.4 | async-start | bytes 131072 | tf_op jit(solution)/shard_map/psum | solution.py:13
  308.4 102.6 %all-reduce.11.cloned.1.call-start = ((), (), s32[]{:S(2)}) async-start(), calls=%async_computation.5 | async-start | bytes 131072 | tf_op jit(solution)/shard_map/psum | solution.py:13
Sparse Core Ops, SparseCore 0:
  177.9 130.4 all-reduce.6
  310.7 58.4 all-reduce.8
  371.8 39.1 all-reduce.10
